TPU v7x, 32 devices: a whole 2x2x4 slice. The times are simulated.
32 devices in a mesh: dp: 8 (over z, y), tensor: 4 (over x, core).
Axes of the slice: x: 2, y: 2, z: 4, core: 2. Of those that a mesh axis runs over, the one named last changes fastest.
Arguments:
- cotangent: bfloat16 [2048, 8192], P(('dp', 'tensor')), may hold values from -1.1048543 to 1.1048543
- gate_pre: bfloat16 [2048, 14336], P('dp', 'tensor'), may hold values from -5 to 5
- up_pre: bfloat16 [2048, 14336], P('dp', 'tensor'), may hold values from -28 to 28
- row_state: float32 [8192], P('dp'), may hold values from 0.02 to 3
- column_state: float32 [14336], P('tensor'), may hold values from 0.05 to 2
Outputs:
- update: float32 [8192, 14336], P('dp', 'tensor')
- row_next: float32 [8192], P('dp')
- column_next: float32 [14336], P('tensor')
- row_scale: float32 [1], replicated
All inputs are finite; a program needn't handle non-finite values.
Results may differ from a plain program's by a relative error of at most 0.019.
Values may be sent and summed in bfloat16 or wider, within the bound.
A program may use at most 192 MiB of HBM per device.

v0:
```python
import jax
import jax.numpy as jnp
from jax import lax
from jax.sharding import PartitionSpec as P

D = 8192
FF = 14336


EPSILON = 1e-30
DECAY_RATE = 0.9


def shards(cotangent, gate_pre, up_pre, row_state, column_state):
    hidden = (jax.nn.silu(gate_pre.astype(jnp.float32)) * up_pre.astype(jnp.float32)).astype(
        jnp.bfloat16
    )
    data_count = lax.axis_size("dp")
    tensor_count = lax.axis_size("tensor")
    spread = lax.all_to_all(cotangent, "dp", split_axis=1, concat_axis=0, tiled=True)
    tokens_all = lax.all_gather(spread, "tensor", axis=0, tiled=True)
    rows_each = cotangent.shape[0]
    block_rows = hidden.shape[0]
    blocks = tokens_all.reshape(tensor_count, data_count, rows_each, tokens_all.shape[1])
    incoming = lax.all_gather(hidden, "dp", axis=0, tiled=True)
    groups = incoming.shape[0] // block_rows
    shaped = incoming.reshape(groups, tensor_count, rows_each, incoming.shape[1])
    partial_value = jnp.einsum("jntd,njtf->ndf", blocks, shaped, preferred_element_type=jnp.float32)
    rounded = lax.optimization_barrier(partial_value.astype(jnp.bfloat16))
    gradient = jnp.sum(rounded.astype(jnp.float32), axis=0)
    squares = gradient * gradient + EPSILON
    column_part = jnp.sum(squares, axis=0)
    row_total = lax.psum(jnp.sum(squares, axis=1), "tensor")
    row_next = DECAY_RATE * row_state + (1.0 - DECAY_RATE) * row_total / FF
    column_total = lax.psum(column_part, "dp")
    row_sum_all = lax.psum(jnp.sum(row_next), "dp")
    column_next = DECAY_RATE * column_state + (1.0 - DECAY_RATE) * column_total / D
    row_mean = row_sum_all / D
    second_moment = row_next[:, None] * column_next[None, :] / row_mean
    raw_update = gradient / jnp.sqrt(second_moment)
    square_total = lax.psum(jnp.sum(raw_update * raw_update), ("dp", "tensor"))
    norm_value = jnp.sqrt(square_total / (float(D) * float(FF)))
    update = raw_update / jnp.maximum(1.0, norm_value)
    return (update, row_next, column_next, jnp.reshape(row_mean, (1,)))


def solution(mesh):
    return jax.shard_map(
        shards,
        mesh=mesh,
        in_specs=(
            P(("dp", "tensor"), None),
            P("dp", "tensor"),
            P("dp", "tensor"),
            P("dp"),
            P("tensor"),
        ),
        out_specs=(P("dp", "tensor"), P("dp"), P("tensor"), P()),
        check_vma=False,
    )
```

profile of v0, /device:TPU:0, one launch (start us, length us, event | category | flops | bytes accessed | tf_op | source)
XLA Modules:
  0.0 464.3 jit_solution(13334387134886437163)
XLA Ops:
  7.2 0.0 all-gather.5.cloned.1.call-start
  7.2 1.3 copy.20
  8.5 33.0 %all_to_all.19 = bf16[64,8,1024]{2,0,1:T(8,128)(2,1)} all-to-all(bf16[64,8,1024]{2,0,1:T(8,128)(2,1)S(1)} %bitcast.19), channel_id=1, replica_groups=mesh['dp'=8,'tensor'=4] {'dp'}, dimensions={1} | all-to-all | bytes 2097152 | tf_op jit(solution)/shard_map/all_to_all | solution.py:20
  41.5 0.0 all-gather.5.cloned.1.call-update
  41.5 0.0 all-gather.3.cloned.1.call-start
  41.6 4.4 fusion.8
  46.0 0.0 all-gather.3.cloned.1.call-update
  46.0 29.2 %all-gather.5.cloned.1.call-done = bf16[2048,1024]{1,0:T(8,128)(2,1)} async-done(((bf16[512,1024]{1,0:T(8,128)(2,1)}), bf16[2048,1024]{1,0:T(8,128)(2,1)}) %all-gather.5.cloned.1.call-update) | async-done | bytes 4194320 | tf_op jit(solution)/shard_map/all_gather | solution.py:21
  75.1 204.5 %all-gather.3.cloned.1.call-done = bf16[2048,3584]{1,0:T(8,128)(2,1)} async-done(((bf16[256,3584]{1,0:T(8,128)(2,1)}), bf16[2048,3584]{1,0:T(8,128)(2,1)}) %all-gather.3.cloned.1.call-update) | async-done | bytes 14680080 | tf_op jit(solution)/shard_map/all_gather | solution.py:25
  279.6 28.0 %fusion = bf16[8,1024,3584]{1,2,0:T(8,128)(2,1)} fusion(bf16[8,4,64,3584]{3,2,1,0:T(8,128)(2,1)} %bitcast.21, bf16[4,8,64,1024]{3,2,1,0:T(8,128)(2,1)} %bitcast.22), kind=kOutput, calls=%fused_computation.2 | convolution fusion | flops 15061745664 | bytes 77594624 | tf_op jit(solution)/shard_map/jntd,njtf->ndf/dot_general | solution.py:28
  307.6 24.8 %convert_reduce_fusion = f32[1024,3584]{0,1:T(8,128)} fusion(bf16[8,1024,3584]{1,2,0:T(8,128)(2,1)} %fusion), kind=kLoop, calls=%fused_computation.1 | loop fusion | flops 55050240 | bytes 73400320 | tf_op jit(solution)/shard_map/reduce_sum | solution.py:30
  332.4 7.7 %fusion.1 = (f32[3584]{0:T(1024)S(1)}, f32[1024]{0:T(1024)S(1)}) fusion(f32[1024,3584]{0,1:T(8,128)} %convert_reduce_fusion), kind=kLoop, calls=%fused_computation.6 | loop fusion | flops 14675456 | bytes 14698496 | tf_op jit(solution)/shard_map/reduce_sum | solution.py:32
  340.1 5.9 %psum.28 = f32[1024]{0:T(1024)S(1)} all-reduce(f32[1024]{0:T(1024)S(1)} %get-tuple-element.9), channel_id=1, replica_groups=mesh['dp'=8,'tensor'=4] {'tensor'}, use_global_device_ids=true, to_apply=%region_2.3 | all-reduce | flops 1024 | bytes 8192 | tf_op jit(solution)/shard_map/psum | solution.py:33
  345.9 0.0 copy-done.3
  345.9 0.6 fusion.9
  346.5 36.4 %all-reduce = (f32[]{:T(128)}, f32[3584]{0:T(1024)S(1)}) all-reduce(f32[]{:T(128)} %get-tuple-element.12, f32[3584]{0:T(1024)S(1)} %get-tuple-element.8), channel_id=1, replica_groups=mesh['dp'=8,'tensor'=4] {'dp'}, use_global_device_ids=true, to_apply=%region_6.7 | all-reduce | flops 3585 | bytes 28680 | tf_op jit(solution)/shard_map/psum | solution.py:36
  383.5 0.0 copy-done.2
  383.6 0.0 copy-start
  383.6 9.4 %multiply_reduce_fusion = f32[]{:T(128)} fusion(f32[1024,3584]{0,1:T(8,128)} %convert_reduce_fusion, f32[]{:T(128)} %div.42, f32[3584]{0:T(1024)S(1)} %multiply_add_fusion.1, f32[1024]{0:T(1024)S(1)} %get-tuple-element.13), kind=kLoop, calls=%fused_computation.3 | loop fusion | flops 18350080 | bytes 14698504 | tf_op jit(solution)/shard_map/reduce_sum | solution.py:41
  392.9 37.1 %psum.31 = f32[]{:T(128)} all-reduce(f32[]{:T(128)} %multiply_reduce_fusion), channel_id=1, replica_groups=mesh['dp'=8,'tensor'=4] {'dp','tensor'}, use_global_device_ids=true, to_apply=%region_8.9 | all-reduce | flops 1 | bytes 8 | tf_op jit(solution)/shard_map/psum | solution.py:41
  430.7 11.3 %broadcast_divide_fusion = f32[1024,3584]{0,1:T(8,128)} fusion(f32[]{:T(128)S(6)} %max_shard_map.3, f32[1024,3584]{0,1:T(8,128)} %convert_reduce_fusion, f32[]{:T(128)} %div.42, f32[3584]{0:T(1024)S(1)} %multiply_add_fusion.1, f32[1024]{0:T(1024)S(1)} %get-tuple-element.13), kind=kLoop, calls=%fused_computation.8 | loop fusion | flops 14680064 | bytes 29378568 | tf_op jit(solution)/shard_map/div | solution.py:43
  442.0 0.0 copy-done.1
  442.0 0.0 copy-done
  442.0 14.3 %copy.14 = f32[1024,3584]{1,0:T(8,128)} copy(f32[1024,3584]{0,1:T(8,128)} %broadcast_divide_fusion) | data formatting | bytes 29360128
  (4 shorter events, 0.0 us)
Async XLA Ops:
  7.2 68.0 %all-gather.5.cloned.1.call-start = ((), (), s32[]{:S(2)}) async-start(), calls=%async_computation.2 | async-start | bytes 5242880 | tf_op jit(solution)/shard_map/all_gather | solution.py:21
  41.5 238.1 %all-gather.3.cloned.1.call-start = ((), (), s32[]{:S(2)}) async-start(), calls=%async_computation.1 | async-start | bytes 16515072 | tf_op jit(solution)/shard_map/all_gather | solution.py:25
  332.4 13.5 %copy-start.3 = (f32[1024]{0:T(1024)S(1)}, f32[1024]{0:T(1024)}, u32[]{:S(2)}) copy-start(f32[1024]{0:T(1024)} %param.8) | copy-start | bytes 12292
  332.4 51.1 %copy-start.2 = (f32[3584]{0:T(1024)S(1)}, f32[3584]{0:T(1024)}, u32[]{:S(2)}) copy-start(f32[3584]{0:T(1024)} %param.9) | copy-start | bytes 43012
  346.5 95.5 %copy-start.1 = (f32[1024]{0:T(1024)}, f32[1024]{0:T(1024)S(1)}, u32[]{:S(2)}) copy-start(f32[1024]{0:T(1024)S(1)} %get-tuple-element.13) | copy-start | bytes 12292
  383.6 58.5 %copy-start = (f32[3584]{0:T(1024)}, f32[3584]{0:T(1024)S(1)}, u32[]{:S(2)}) copy-start(f32[3584]{0:T(1024)S(1)} %multiply_add_fusion.1) | copy-start | bytes 43012
Sparse Core Ops, SparseCore 0:
  41.6 33.4 all-gather.4
  77.9 201.6 all-gather.2
where the time goes:
time: 466 us; the launch traced here: 464 us
  waiting for transfers between devices  234 us (50%)
  blocking collectives  112 us (24%)
  other arithmetic  58.1 us (12%)
  matrix products  28 us (6%)
  between operations  16.6 us (4%)
  local copies, waits for them, and re-layouts  15.6 us (3%)
    all_gather x1, waiting for transfers between devices, shards(): incoming = lax.all_gather(hidden, 'dp', axis=0, tiled=True)  204 us
    psum x1, blocking collectives, shards(): square_total = lax.psum(jnp.sum(raw_update * raw_update), ('dp', 'tensor'))  37.1 us
    psum x1, blocking collectives, shards(): row_sum_all = lax.psum(jnp.sum(row_next), 'dp')  36.4 us
    all_to_all x1, blocking collectives, shards(): lax.all_to_all(cotangent, 'dp', split_axis=1, concat_axis=0, tiled=True)  33 us
    all_gather x1, waiting for transfers between devices, shards(): tokens_all = lax.all_gather(spread, 'tensor', axis=0, tiled=True)  29.2 us
    dot_general x1, matrix products, shards(): jnp.einsum('jntd,njtf->ndf', blocks, shaped, preferred_element_type=jnp.f...  28 us
    reduce_sum x1, other arithmetic, shards(): gradient = jnp.sum(rounded.astype(jnp.float32), axis=0)  24.8 us
    unnamed x9, local copies, waits for them, and re-layouts  14.3 us
  transfers between devices with their start and end apart: 2, of which 2 were waited for; matrix products, arithmetic and copies ran while one was open for 1% of the time, Pallas kernels for 0%

commit v1 on v0

v1 whole, which is shorter than its diff:
```python
import functools

import jax
import jax.numpy as jnp
from jax import lax
from jax.experimental import pallas as pl
from jax.experimental.pallas import tpu as pltpu
from jax.sharding import PartitionSpec as P

EPSILON = 1e-30
DECAY_RATE = 0.9
MESH = pl.DeviceIdType.MESH
PAIR = 2
LAG = 2


def chunk_count(width):
    for count in (7, 8, 6, 5, 4, 3, 2):
        if width % (count * 128) == 0:
            return count
    return 1


def kernel(
    n_dp, n_t, chunks, rows_all, cols_all,
    cot, gate, up, row_state, column_state,
    g_out, row_out, col_out, rfac_out, cfac_out, mean_out,
    hid, cr, cot_t, grad, row_part, col_part, rbuf, cbuf, pbuf, qbuf,
    own_sem, a2a_s, a2a_r, ag_s, ag_r, hs, hr, g_sem, rs, rr, cs, cr_sem, ps, pr, qs, qr,
):
    me = lax.axis_index("dp")
    tt = lax.axis_index("tensor")
    line = n_dp // PAIR
    i = me // PAIR
    j = me % PAIR
    other = i * PAIR + (1 - j)
    width = cr.shape[3]
    tokens = hid.shape[2]
    fc = hid.shape[3]

    barrier = pltpu.get_barrier_semaphore()
    for off in range(1, n_dp):
        pl.semaphore_signal(barrier, inc=1, device_id=((me + off) % n_dp, tt), device_id_type=MESH)
    for off in range(1, n_t):
        pl.semaphore_signal(barrier, inc=1, device_id=(me, (tt + off) % n_t), device_id_type=MESH)
    pl.semaphore_wait(barrier, n_dp + n_t - 2)

    def a2a(off):
        d = (me + off) % n_dp
        return pltpu.make_async_remote_copy(
            cot.at[:, pl.ds(pl.multiple_of(d * width, width), width)],
            cr.at[me, tt], a2a_s.at[d], a2a_r.at[me],
            device_id=(d, tt), device_id_type=MESH)

    def a2a_in(off):
        g = (me + off) % n_dp
        return pltpu.make_async_remote_copy(
            cr.at[g, tt], cr.at[g, tt], a2a_s.at[g], a2a_r.at[g],
            device_id=(g, tt), device_id_type=MESH)

    def gather(off):
        t = (tt + off) % n_t
        return pltpu.make_async_remote_copy(
            cr.at[:, tt], cr.at[:, tt], ag_s.at[t], ag_r.at[tt],
            device_id=(me, t), device_id_type=MESH)

    def gather_in(off):
        t = (tt + off) % n_t
        return pltpu.make_async_remote_copy(
            cr.at[:, t], cr.at[:, t], ag_s.at[t], ag_r.at[t],
            device_id=(me, t), device_id_type=MESH)

    def move(way, c, g):
        to = (me - PAIR, me + PAIR, other)[way]
        return pltpu.make_async_remote_copy(
            hid.at[c, g], hid.at[c, g], hs.at[way, c, g], hr.at[c, g],
            device_id=(to, tt), device_id_type=MESH)

    def send_left(c, g):
        @pl.when(i > 0)
        def _():
            move(0, c, g).start()

    def send_right(c, g):
        @pl.when(i < line - 1)
        def _():
            move(1, c, g).start()

    def arrived(c, g):
        move(2, c, g).wait_recv()

    own = pltpu.make_async_copy(
        cot.at[:, pl.ds(pl.multiple_of(me * width, width), width)], cr.at[me, tt], own_sem)
    own.start()
    for off in range(1, n_dp):
        a2a(off).start()

    for c in range(chunks):
        v = gate[:, c * fc:(c + 1) * fc].astype(jnp.float32)
        u = up[:, c * fc:(c + 1) * fc].astype(jnp.float32)
        hid[c, me] = (v / (1.0 + jnp.exp(-v)) * u).astype(jnp.bfloat16)
    own.wait()

    move(2, 0, me).start()

    @pl.loop(1, chunks)
    def _(c):
        send_left(c, me)
        send_right(c, me)
        move(2, c, me).start()

    send_left(0, me)
    send_right(0, me)

    row_part[...] = jnp.zeros_like(row_part)
    col_part[...] = jnp.zeros_like(col_part)

    for off in range(1, n_dp):
        a2a_in(off).wait_recv()
    for off in range(1, n_t):
        gather(off).start()

    arrived(0, other)
    send_left(0, other)
    send_right(0, other)

    def turn(g):
        block = cr[g].reshape(tokens, width)
        cot_t[:, pl.ds(pl.multiple_of(g * tokens, 128), tokens)] = block.T

    tile = min(256, width)

    def product(c):
        @pl.loop(0, n_dp)
        def _(g):
            @pl.when((g % PAIR != j) & (c > 0))
            def _():
                arrived(c, g)

        @pl.loop(0, width // tile)
        def _(m):
            at = pl.ds(pl.multiple_of(m * tile, tile), tile)
            value = jnp.dot(cot_t[at, :], hid[c].reshape(n_dp * tokens, fc),
                            preferred_element_type=jnp.float32)
            grad[c, at, :] = value
            square = value * value + EPSILON
            col_part[c] += jnp.sum(square.reshape(tile // 8, 8, fc), axis=0)
            lanes = square[:, 0:128]
            for k in range(1, fc // 128):
                lanes = lanes + square[:, k * 128:(k + 1) * 128]
            row_part[at, :] += lanes

    def put(c):
        return pltpu.make_async_copy(grad.at[c], g_out.at[:, c * fc:(c + 1) * fc], g_sem.at[c])

    turn_hop = max(1, line - 2)
    per = -(-n_dp // max(1, chunks - 1))
    for h in range(1, line):
        last = h == line - 1
        gl = me - h * PAIR
        gr = me + h * PAIR

        def step(c, h=h, gl=gl, gr=gr):
            @pl.when(i >= h)
            def _():
                arrived(c, gl)
                send_right(c, gl)
                move(2, c, gl).start()

            @pl.when(i + h < line)
            def _():
                arrived(c, gr)
                send_left(c, gr)
                move(2, c, gr).start()

        for c in range(1, chunks):
            step(c)
            if h == turn_hop:
                if c == 1:
                    for off in range(1, n_t):
                        gather_in(off).wait_recv()
                for g in range((c - 1) * per, min(c * per, n_dp)):
                    turn(g)
            if last and c - LAG >= 1:
                product(c - LAG)
        for jj in (j, 1 - j):
            ql = (i - h) * PAIR + jj
            qr_ = (i + h) * PAIR + jj

            @pl.when(i >= h)
            def _():
                arrived(0, ql)
                send_right(0, ql)

            @pl.when(i + h < line)
            def _():
                arrived(0, qr_)
                send_left(0, qr_)

    if chunks == 1:
        for off in range(1, n_t):
            gather_in(off).wait_recv()
        for g in range(n_dp):
            turn(g)
    for c in range(max(1, chunks - LAG), chunks):
        product(c)
    product(0)

    rbuf[tt] = jnp.sum(row_part[...].T, axis=0, keepdims=True)
    for c in range(chunks):
        cbuf[me, c] = jnp.sum(col_part[c], axis=0, keepdims=True)

    def rmove(off, mine):
        t = (tt + off) % n_t
        k = tt if mine else t
        return pltpu.make_async_remote_copy(
            rbuf.at[k], rbuf.at[k], rs.at[t], rr.at[k], device_id=(me, t), device_id_type=MESH)

    def cmove(off, mine):
        d = (me + off) % n_dp
        k = me if mine else d
        return pltpu.make_async_remote_copy(
            cbuf.at[k], cbuf.at[k], cs.at[d], cr_sem.at[k], device_id=(d, tt), device_id_type=MESH)

    def pmove(off, mine):
        t = (tt + off) % n_t
        k = tt if mine else t
        return pltpu.make_async_remote_copy(
            pbuf.at[k], pbuf.at[k], ps.at[t], pr.at[k], device_id=(me, t), device_id_type=MESH)

    def qmove(off, mine):
        d = (me + off) % n_dp
        k = me if mine else d
        return pltpu.make_async_remote_copy(
            qbuf.at[k], qbuf.at[k], qs.at[d], qr.at[k], device_id=(d, tt), device_id_type=MESH)

    for off in range(1, n_dp):
        cmove(off, True).start()
    for off in range(1, n_t):
        rmove(off, True).start()
    for c in range(chunks):
        put(c).start()

    @pl.loop(0, chunks)
    def _(c):
        @pl.loop(0, n_dp)
        def _(g):
            gi = g // PAIR
            mine = g % PAIR == j

            @pl.when((i > 0) & (gi >= i) & (mine | (c == 0)))
            def _():
                move(0, c, g).wait_send()

            @pl.when((i < line - 1) & (gi <= i) & (mine | (c == 0)))
            def _():
                move(1, c, g).wait_send()

            @pl.when(mine & ((gi == i) | (c > 0)))
            def _():
                move(2, c, g).wait_send()

    for off in range(1, n_dp):
        a2a(off).wait_send()
    for off in range(1, n_t):
        gather(off).wait_send()

    for off in range(1, n_t):
        rmove(off, False).wait_recv()
    row_total = rbuf[0]
    for t in range(1, n_t):
        row_total = row_total + rbuf[t]
    row_next = DECAY_RATE * row_state[...] + (1.0 - DECAY_RATE) * (row_total / cols_all)
    row_out[...] = row_next
    weight = 1.0 / row_next
    row_part[...] = jnp.broadcast_to(weight, (128, width)).T

    for off in range(1, n_dp):
        cmove(off, False).wait_recv()
    total = jnp.zeros((8, fc), jnp.float32)
    for c in range(chunks):
        col_total = cbuf[0, c]
        for d in range(1, n_dp):
            col_total = col_total + cbuf[d, c]
        col_next = DECAY_RATE * column_state[c] + (1.0 - DECAY_RATE) * (col_total / rows_all)
        col_out[c] = col_next

        def body(m, carry, c=c):
            at = pl.ds(pl.multiple_of(m * tile, tile), tile)
            w = row_part[at, :]
            parts = []
            for k in range(fc // 128):
                value = grad[c, at, k * 128:(k + 1) * 128]
                parts.append(jnp.sum((value * value * w).reshape(tile // 8, 8, 128), axis=0))
            return carry + jnp.concatenate(parts, axis=1)

        weighted = lax.fori_loop(0, width // tile, body, jnp.zeros((8, fc), jnp.float32))
        total = total + weighted * (1.0 / col_next)

    def whole_sum(x):
        return jnp.sum(jnp.sum(x, axis=1, keepdims=True), axis=0, keepdims=True)

    pbuf[tt] = jnp.broadcast_to(whole_sum(total), (8, 128))
    for off in range(1, n_t):
        pmove(off, True).start()
    row_sum = whole_sum(row_next)
    for off in range(1, n_t):
        pmove(off, False).wait_recv()
    square_sum = pbuf[0]
    for t in range(1, n_t):
        square_sum = square_sum + pbuf[t]
    qbuf[me, 0:8] = square_sum
    qbuf[me, 8:16] = jnp.broadcast_to(row_sum, (8, 128))
    for off in range(1, n_dp):
        qmove(off, True).start()
    for off in range(1, n_dp):
        qmove(off, False).wait_recv()
    sums = qbuf[0]
    for d in range(1, n_dp):
        sums = sums + qbuf[d]
    mean = sums[8:9, 0:1] / rows_all
    norm = jnp.sqrt(mean * (sums[0:1, 0:1] / rows_all / cols_all))
    factor = jnp.sqrt(mean) / jnp.maximum(1.0, norm)
    mean_out[...] = jnp.broadcast_to(mean, (1, 128))
    rfac_out[...] = factor * lax.rsqrt(row_next)
    for c in range(chunks):
        cfac_out[c] = lax.rsqrt(col_out[c])

    for off in range(1, n_dp):
        cmove(off, True).wait_send()
        qmove(off, True).wait_send()
    for off in range(1, n_t):
        rmove(off, True).wait_send()
        pmove(off, True).wait_send()
    for c in range(chunks):
        put(c).wait()


def solution(mesh):
    n_dp, n_t = mesh.shape["dp"], mesh.shape["tensor"]

    def shards(cotangent, gate_pre, up_pre, row_state, column_state):
        rows_each, d_all = cotangent.shape
        tokens, ff = gate_pre.shape
        width = row_state.shape[0]
        chunks = chunk_count(ff)
        fc = ff // chunks
        f32, bf16 = jnp.float32, jnp.bfloat16
        dma, vmem = pltpu.SemaphoreType.DMA, pltpu.VMEM
        spec = pl.BlockSpec(memory_space=pltpu.VMEM)
        grad, row_next, col_next, rfac, cfac, mean = pl.pallas_call(
            functools.partial(kernel, n_dp, n_t, chunks, float(d_all), float(ff * n_t)),
            out_shape=(
                jax.ShapeDtypeStruct((width, ff), f32),
                jax.ShapeDtypeStruct((1, width), f32),
                jax.ShapeDtypeStruct((chunks, 1, fc), f32),
                jax.ShapeDtypeStruct((1, width), f32),
                jax.ShapeDtypeStruct((chunks, 1, fc), f32),
                jax.ShapeDtypeStruct((1, 128), f32),
            ),
            in_specs=[spec] * 5,
            out_specs=(pl.BlockSpec(memory_space=pl.ANY),) + (spec,) * 5,
            scratch_shapes=[
                vmem((chunks, n_dp, tokens, fc), bf16),
                vmem((n_dp, n_t, rows_each, width), bf16),
                vmem((width, n_dp * tokens), bf16),
                vmem((chunks, width, fc), f32),
                vmem((width, 128), f32),
                vmem((chunks, 8, fc), f32),
                vmem((n_t, 1, width), f32),
                vmem((n_dp, chunks, 1, fc), f32),
                vmem((n_t, 8, 128), f32),
                vmem((n_dp, 16, 128), f32),
                dma, dma((n_dp,)), dma((n_dp,)), dma((n_t,)), dma((n_t,)),
                dma((3, chunks, n_dp)), dma((chunks, n_dp)), dma((chunks,)),
                dma((n_t,)), dma((n_t,)), dma((n_dp,)), dma((n_dp,)),
                dma((n_t,)), dma((n_t,)), dma((n_dp,)), dma((n_dp,)),
            ],
            compiler_params=pltpu.CompilerParams(
                collective_id=0, has_side_effects=True, vmem_limit_bytes=60 * 1024 * 1024),
        )(cotangent, gate_pre, up_pre, row_state.reshape(1, width),
          column_state.reshape(chunks, 1, fc))
        update = grad * rfac.reshape(width)[:, None] * cfac.reshape(ff)[None, :]
        return (update, row_next.reshape(width), col_next.reshape(ff), mean[0, 0:1])

    return jax.shard_map(
        shards,
        mesh=mesh,
        in_specs=(
            P(("dp", "tensor"), None),
            P("dp", "tensor"),
            P("dp", "tensor"),
            P("dp"),
            P("tensor"),
        ),
        out_specs=(P("dp", "tensor"), P("dp"), P("tensor"), P()),
        check_vma=False,
    )
```

time: 466 us -> 206 us (0.44)
  waiting for transfers between devices: 234 us -> 0 us
  Pallas kernels: 0 us -> 188 us
  blocking collectives: 112 us -> 0 us
  other arithmetic: 58.1 us -> 13.6 us
  matrix products: 28 us -> 0 us
  between operations: 16.6 us -> 1.85 us
  local copies, waits for them, and re-layouts: 15.6 us -> 2.55 us
    all_gather x2 -> x0, waiting for transfers between devices: 234 us -> none  [the longest x1 204 us: shards(): incoming = lax.all_gather(hidden, 'dp', axis=0, tiled=True)]
    pallas_call x0 -> x1, Pallas kernels: none -> 188 us  [shards(): pl.pallas_call(functools.partial(kernel, n_dp, n_t, chunks, float(d_all),...]
    psum x3 -> x0, blocking collectives: 79.3 us -> none  [the longest x1 37.1 us: shards(): square_total = lax.psum(jnp.sum(raw_update * raw_update), ('dp', 'tensor'))]
    reduce_sum x4 -> x0, other arithmetic: 42.4 us -> none  [the longest x1 24.8 us: shards(): gradient = jnp.sum(rounded.astype(jnp.float32), axis=0)]
    all_to_all x1 -> x0, blocking collectives: 33 us -> none  [shards(): lax.all_to_all(cotangent, 'dp', split_axis=1, concat_axis=0, tiled=True)]
    dot_general x1 -> x0, matrix products: 28 us -> none  [shards(): jnp.einsum('jntd,njtf->ndf', blocks, shaped, preferred_element_type=jnp.f...]
    unnamed x9 -> x7, local copies, waits for them, and re-layouts: 14.3 us -> 0.61 us
    mul x0 -> x1, other arithmetic: none -> 12.8 us  [shards(): update = grad * rfac.reshape(width)[:, None] * cfac.reshape(ff)[None, :]]
  transfers between devices with their start and end apart: 2 -> 0, of which waited for: 2 -> 0; matrix products, arithmetic and copies ran while one was open for 1% -> 0% of each run, Pallas kernels for 0% -> 0%
where the time goes in v1:
time: 206 us
  Pallas kernels  188 us (91%)
  other arithmetic  13.6 us (7%)
  local copies, waits for them, and re-layouts  2.55 us (1%)
    pallas_call x1, Pallas kernels, shards(): pl.pallas_call(functools.partial(kernel, n_dp, n_t, chunks, float(d_all),...  188 us
    mul x1, other arithmetic, shards(): update = grad * rfac.reshape(width)[:, None] * cfac.reshape(ff)[None, :]  12.8 us

profile of v1, /device:TPU:0, one launch (start us, length us, event | category | flops | bytes accessed | tf_op | source)
XLA Modules:
  0.0 205.8 jit_solution(11693245883483416899)
XLA Ops:
  0.6 1.3 reshape.23.column_state
  2.0 187.8 %shard_map.84 = (f32[1024,3584]{1,0:T(8,128)}, f32[1,1024]{1,0:T(1,128)}, f32[7,1,512]{2,1,0:T(1,128)}, f32[1,1024]{1,0:T(1,128)}, f32[7,1,512]{2,1,0:T(1,128)}, /*index=5*/f32[1,128]{1,0:T(1,128)}) custom-call(bf16[64,8192]{1,0:T(8,128)(2,1)} %cot.1, bf16[256,3584]{1,0:T(8,128)(2,1)} %gate.1, bf16[256,3584]{1,0:T(8,128)(2,1)} %up.1, f32[1,1024]{1,0:T(1,128)} %bitcast.7, ...), custom_call_target="tpu_custom_call" | custom-call | tf_op jit(solution)/shard_map/pallas_call | solution.py:351
  189.8 0.8 reduce
  190.6 0.0 copy-start
  190.6 0.0 copy-start.1
  190.6 0.0 copy-start.2
  190.6 12.8 %multiply_multiply_fusion = f32[1024,3584]{1,0:T(8,128)} fusion(f32[1024,3584]{1,0:T(8,128)} %get-tuple-element.10, f32[3584]{0:T(1024)S(1)} %mul.23, f32[1024]{0:T(1024)} %bitcast.5), kind=kLoop, calls=%fused_computation | loop fusion | flops 7340032 | bytes 29378560 | tf_op jit(solution)/shard_map/mul | solution.py:383
  203.4 0.0 copy-done
  203.4 0.6 reshape.25
  204.0 0.0 copy-done.1
  204.0 0.6 copy.11
  204.6 0.0 copy-done.2
  (2 shorter events, 0.0 us)
Async XLA Ops:
  190.6 12.8 %copy-start = (f32[7,1,512]{2,1,0:T(1,128)S(1)}, f32[7,1,512]{2,1,0:T(1,128)}, u32[]{:S(2)}) copy-start(f32[7,1,512]{2,1,0:T(1,128)} %get-tuple-element.14) | copy-start | bytes 43012
  190.6 13.5 %copy-start.1 = (f32[1,1024]{1,0:T(1,128)S(1)}, f32[1,1024]{1,0:T(1,128)}, u32[]{:S(2)}) copy-start(f32[1,1024]{1,0:T(1,128)} %get-tuple-element.13) | copy-start | bytes 12292
  190.6 14.0 %copy-start.2 = (f32[1,128]{1,0:T(1,128)S(1)}, f32[1,128]{1,0:T(1,128)}, u32[]{:S(2)}) copy-start(f32[1,128]{1,0:T(1,128)} %get-tuple-element.15) | copy-start | bytes 1540

commit v2 on v1

--- a/solution.py
+++ b/solution.py
@@ -12,6 +12,7 @@
 MESH = pl.DeviceIdType.MESH
 PAIR = 2
 LAG = 2
+GRANT = 46
 
 
 def chunk_count(width):
@@ -23,10 +24,10 @@
 
 def kernel(
     n_dp, n_t, chunks, rows_all, cols_all,
-    cot, gate, up, row_state, column_state,
-    g_out, row_out, col_out, rfac_out, cfac_out, mean_out,
-    hid, cr, cot_t, grad, row_part, col_part, rbuf, cbuf, pbuf, qbuf,
-    own_sem, a2a_s, a2a_r, ag_s, ag_r, hs, hr, g_sem, rs, rr, cs, cr_sem, ps, pr, qs, qr,
+    cot, gate_in, up_in, row_state, column_state,
+    grad, row_out, col_out, rfac_out, cfac_out, mean_out,
+    gate, up, hid, cr, cot_t, row_part, col_part, rbuf, cbuf, pbuf, qbuf,
+    own_sem, load_sem, a2a_s, a2a_r, ag_s, ag_r, hs, hr, rs, rr, cs, cr_sem, ps, pr, qs, qr,
 ):
     me = lax.axis_index("dp")
     tt = lax.axis_index("tensor")
@@ -38,6 +39,11 @@
     tokens = hid.shape[2]
     fc = hid.shape[3]
 
+    loads = [pltpu.make_async_copy(gate_in, gate, load_sem.at[0]),
+             pltpu.make_async_copy(up_in, up, load_sem.at[1])]
+    for load in loads:
+        load.start()
+
     barrier = pltpu.get_barrier_semaphore()
     for off in range(1, n_dp):
         pl.semaphore_signal(barrier, inc=1, device_id=((me + off) % n_dp, tt), device_id_type=MESH)
@@ -95,6 +101,8 @@
     for off in range(1, n_dp):
         a2a(off).start()
 
+    for load in loads:
+        load.wait()
     for c in range(chunks):
         v = gate[:, c * fc:(c + 1) * fc].astype(jnp.float32)
         u = up[:, c * fc:(c + 1) * fc].astype(jnp.float32)
@@ -130,31 +138,68 @@
 
     tile = min(256, width)
 
-    def product(c):
-        @pl.loop(0, n_dp)
-        def _(g):
-            @pl.when((g % PAIR != j) & (c > 0))
-            def _():
-                arrived(c, g)
+    late = min(PAIR, n_dp)
+    early = n_dp - late
+    low = (i < (line + 1) // 2).astype(jnp.int32)
+    early_at = (1 - low) * late
+    late_at = low * early
+
+    def multiply(c, first, count, fresh, final):
+        cols = slice(c * fc, (c + 1) * fc)
+        depth = pl.ds(pl.multiple_of(first * tokens, 128), count * tokens)
 
         @pl.loop(0, width // tile)
         def _(m):
             at = pl.ds(pl.multiple_of(m * tile, tile), tile)
-            value = jnp.dot(cot_t[at, :], hid[c].reshape(n_dp * tokens, fc),
+            value = jnp.dot(cot_t[at, depth], hid[c, pl.ds(first, count)].reshape(count * tokens, fc),
                             preferred_element_type=jnp.float32)
-            grad[c, at, :] = value
-            square = value * value + EPSILON
-            col_part[c] += jnp.sum(square.reshape(tile // 8, 8, fc), axis=0)
-            lanes = square[:, 0:128]
-            for k in range(1, fc // 128):
-                lanes = lanes + square[:, k * 128:(k + 1) * 128]
-            row_part[at, :] += lanes
-
-    def put(c):
-        return pltpu.make_async_copy(grad.at[c], g_out.at[:, c * fc:(c + 1) * fc], g_sem.at[c])
+            if not fresh:
+                value = value + grad[at, cols]
+            grad[at, cols] = value
+            if final:
+                square = value * value + EPSILON
+                col_part[c] += jnp.sum(square.reshape(tile // 8, 8, fc), axis=0)
+                lanes = square[:, 0:128]
+                for k in range(1, fc // 128):
+                    lanes = lanes + square[:, k * 128:(k + 1) * 128]
+                row_part[at, :] += lanes
+
+    def crossed(c, first, count):
+        if c > 0:
+            for k in range(count // PAIR):
+                arrived(c, first + k * PAIR + (1 - j))
+
+    def product_early(c):
+        if early:
+            crossed(c, early_at, early)
+            multiply(c, early_at, early, True, False)
+
+    def collect(c):
+        @pl.loop(0, n_dp)
+        def _(g):
+            gi = g // PAIR
+            mine = g % PAIR == j
+            z_line = mine if c > 0 else g >= 0
+
+            @pl.when((i > 0) & (gi >= i) & z_line)
+            def _():
+                move(0, c, g).wait_send()
+
+            @pl.when((i < line - 1) & (gi <= i) & z_line)
+            def _():
+                move(1, c, g).wait_send()
+
+            @pl.when(mine if c > 0 else mine & (gi == i))
+            def _():
+                move(2, c, g).wait_send()
+
+    def product_late(c):
+        crossed(c, late_at, late)
+        multiply(c, late_at, late, not early, True)
 
     turn_hop = max(1, line - 2)
-    per = -(-n_dp // max(1, chunks - 1))
+    skip = (chunks - 1) // 2
+    per = -(-n_dp // max(1, chunks - 1 - skip))
     for h in range(1, line):
         last = h == line - 1
         gl = me - h * PAIR
@@ -175,14 +220,23 @@
 
         for c in range(1, chunks):
             step(c)
-            if h == turn_hop:
-                if c == 1:
+            if h == turn_hop and c > skip:
+                if c == skip + 1:
                     for off in range(1, n_t):
                         gather_in(off).wait_recv()
-                for g in range((c - 1) * per, min(c * per, n_dp)):
+                for g in range((c - 1 - skip) * per, min((c - skip) * per, n_dp)):
                     turn(g)
-            if last and c - LAG >= 1:
-                product(c - LAG)
+            if last:
+                if c == 1:
+                    product_early(1)
+                    product_early(2 % chunks)
+                elif c + 1 < chunks:
+                    product_early(c + 1)
+                else:
+                    product_early(0)
+                if c - LAG >= 1:
+                    product_late(c - LAG)
+                    collect(c - LAG)
         for jj in (j, 1 - j):
             ql = (i - h) * PAIR + jj
             qr_ = (i + h) * PAIR + jj
@@ -197,14 +251,9 @@
                 arrived(0, qr_)
                 send_left(0, qr_)
 
-    if chunks == 1:
-        for off in range(1, n_t):
-            gather_in(off).wait_recv()
-        for g in range(n_dp):
-            turn(g)
-    for c in range(max(1, chunks - LAG), chunks):
-        product(c)
-    product(0)
+    for c in range(chunks - LAG, chunks):
+        product_late(c)
+    product_late(0)
 
     rbuf[tt] = jnp.sum(row_part[...].T, axis=0, keepdims=True)
     for c in range(chunks):
@@ -238,28 +287,9 @@
         cmove(off, True).start()
     for off in range(1, n_t):
         rmove(off, True).start()
-    for c in range(chunks):
-        put(c).start()
-
-    @pl.loop(0, chunks)
-    def _(c):
-        @pl.loop(0, n_dp)
-        def _(g):
-            gi = g // PAIR
-            mine = g % PAIR == j
-
-            @pl.when((i > 0) & (gi >= i) & (mine | (c == 0)))
-            def _():
-                move(0, c, g).wait_send()
-
-            @pl.when((i < line - 1) & (gi <= i) & (mine | (c == 0)))
-            def _():
-                move(1, c, g).wait_send()
-
-            @pl.when(mine & ((gi == i) | (c > 0)))
-            def _():
-                move(2, c, g).wait_send()
-
+
+    for c in (0,) + tuple(range(max(1, chunks - LAG), chunks)):
+        collect(c)
     for off in range(1, n_dp):
         a2a(off).wait_send()
     for off in range(1, n_t):
@@ -274,6 +304,19 @@
     row_out[...] = row_next
     weight = 1.0 / row_next
     row_part[...] = jnp.broadcast_to(weight, (128, width)).T
+    rfac_out[...] = jnp.sqrt(row_part[...])
+
+    for c in range(chunks):
+        def body(m, carry, c=c):
+            at = pl.ds(pl.multiple_of(m * tile, tile), tile)
+            w = row_part[at, :]
+            parts = []
+            for k in range(fc // 128):
+                value = grad[at, c * fc + k * 128:c * fc + (k + 1) * 128]
+                parts.append(jnp.sum((value * value * w).reshape(tile // 8, 8, 128), axis=0))
+            return carry + jnp.concatenate(parts, axis=1)
+
+        col_part[c] = lax.fori_loop(0, width // tile, body, jnp.zeros((8, fc), jnp.float32))
 
     for off in range(1, n_dp):
         cmove(off, False).wait_recv()
@@ -282,20 +325,9 @@
         col_total = cbuf[0, c]
         for d in range(1, n_dp):
             col_total = col_total + cbuf[d, c]
-        col_next = DECAY_RATE * column_state[c] + (1.0 - DECAY_RATE) * (col_total / rows_all)
-        col_out[c] = col_next
-
-        def body(m, carry, c=c):
-            at = pl.ds(pl.multiple_of(m * tile, tile), tile)
-            w = row_part[at, :]
-            parts = []
-            for k in range(fc // 128):
-                value = grad[c, at, k * 128:(k + 1) * 128]
-                parts.append(jnp.sum((value * value * w).reshape(tile // 8, 8, 128), axis=0))
-            return carry + jnp.concatenate(parts, axis=1)
-
-        weighted = lax.fori_loop(0, width // tile, body, jnp.zeros((8, fc), jnp.float32))
-        total = total + weighted * (1.0 / col_next)
+        col_next = DECAY_RATE * column_state[:, c * fc:(c + 1) * fc] + (1.0 - DECAY_RATE) * (col_total / rows_all)
+        col_out[:, c * fc:(c + 1) * fc] = col_next
+        total = total + col_part[c] * (1.0 / col_next)
 
     def whole_sum(x):
         return jnp.sum(jnp.sum(x, axis=1, keepdims=True), axis=0, keepdims=True)
@@ -322,9 +354,7 @@
     norm = jnp.sqrt(mean * (sums[0:1, 0:1] / rows_all / cols_all))
     factor = jnp.sqrt(mean) / jnp.maximum(1.0, norm)
     mean_out[...] = jnp.broadcast_to(mean, (1, 128))
-    rfac_out[...] = factor * lax.rsqrt(row_next)
-    for c in range(chunks):
-        cfac_out[c] = lax.rsqrt(col_out[c])
+    cfac_out[...] = factor * lax.rsqrt(col_out[...])
 
     for off in range(1, n_dp):
         cmove(off, True).wait_send()
@@ -332,8 +362,14 @@
     for off in range(1, n_t):
         rmove(off, True).wait_send()
         pmove(off, True).wait_send()
-    for c in range(chunks):
-        put(c).wait()
+
+
+def scale(rows, grad, rfac, cfac, out):
+    at = pl.ds(pl.multiple_of(pl.program_id(0) * rows, rows), rows)
+    row = rfac[at, :]
+    for k in range(grad.shape[1] // 128):
+        cols = slice(k * 128, (k + 1) * 128)
+        out[:, cols] = grad[at, cols] * row * cfac[:, cols]
 
 
 def solution(mesh):
@@ -351,36 +387,45 @@
         grad, row_next, col_next, rfac, cfac, mean = pl.pallas_call(
             functools.partial(kernel, n_dp, n_t, chunks, float(d_all), float(ff * n_t)),
             out_shape=(
-                jax.ShapeDtypeStruct((width, ff), f32),
+                pltpu.VMEM((width, ff), f32),
                 jax.ShapeDtypeStruct((1, width), f32),
-                jax.ShapeDtypeStruct((chunks, 1, fc), f32),
-                jax.ShapeDtypeStruct((1, width), f32),
-                jax.ShapeDtypeStruct((chunks, 1, fc), f32),
+                jax.ShapeDtypeStruct((1, ff), f32),
+                pltpu.VMEM((width, 128), f32),
+                pltpu.VMEM((1, ff), f32),
                 jax.ShapeDtypeStruct((1, 128), f32),
             ),
-            in_specs=[spec] * 5,
-            out_specs=(pl.BlockSpec(memory_space=pl.ANY),) + (spec,) * 5,
+            in_specs=[pl.BlockSpec(memory_space=pl.ANY)] * 3 + [spec] * 2,
+            out_specs=(spec,) * 6,
             scratch_shapes=[
+                vmem((tokens, ff), bf16),
+                vmem((tokens, ff), bf16),
                 vmem((chunks, n_dp, tokens, fc), bf16),
                 vmem((n_dp, n_t, rows_each, width), bf16),
                 vmem((width, n_dp * tokens), bf16),
-                vmem((chunks, width, fc), f32),
                 vmem((width, 128), f32),
                 vmem((chunks, 8, fc), f32),
                 vmem((n_t, 1, width), f32),
                 vmem((n_dp, chunks, 1, fc), f32),
                 vmem((n_t, 8, 128), f32),
                 vmem((n_dp, 16, 128), f32),
-                dma, dma((n_dp,)), dma((n_dp,)), dma((n_t,)), dma((n_t,)),
-                dma((3, chunks, n_dp)), dma((chunks, n_dp)), dma((chunks,)),
+                dma, dma((2,)), dma((n_dp,)), dma((n_dp,)), dma((n_t,)), dma((n_t,)),
+                dma((3, chunks, n_dp)), dma((chunks, n_dp)),
                 dma((n_t,)), dma((n_t,)), dma((n_dp,)), dma((n_dp,)),
                 dma((n_t,)), dma((n_t,)), dma((n_dp,)), dma((n_dp,)),
             ],
             compiler_params=pltpu.CompilerParams(
-                collective_id=0, has_side_effects=True, vmem_limit_bytes=60 * 1024 * 1024),
+                collective_id=0, has_side_effects=True, vmem_limit_bytes=GRANT * 1024 * 1024),
         )(cotangent, gate_pre, up_pre, row_state.reshape(1, width),
-          column_state.reshape(chunks, 1, fc))
-        update = grad * rfac.reshape(width)[:, None] * cfac.reshape(ff)[None, :]
+          column_state.reshape(1, ff))
+        rows = min(128, width)
+        update = pl.pallas_call(
+            functools.partial(scale, rows),
+            out_shape=jax.ShapeDtypeStruct((width, ff), f32),
+            grid=(width // rows,),
+            in_specs=[spec] * 3,
+            out_specs=pl.BlockSpec((rows, ff), lambda m: (m, 0)),
+            compiler_params=pltpu.CompilerParams(vmem_limit_bytes=16 * 1024 * 1024),
+        )(grad, rfac, cfac)
         return (update, row_next.reshape(width), col_next.reshape(ff), mean[0, 0:1])
 
     return jax.shard_map(

time: 206 us -> 191 us (0.927)
  other arithmetic: 13.6 us -> 0.64 us
    mul x1 -> x0, other arithmetic: 12.8 us -> none  [shards(): update = grad * rfac.reshape(width)[:, None] * cfac.reshape(ff)[None, :]]
    pallas_call x1, Pallas kernels: 188 us -> 179 us  [shards(): pl.pallas_call(functools.partial(kernel, n_dp, n_t, chunks, float(d_all),...]
    pallas_call x0 -> x1, Pallas kernels: none -> 6.38 us  [shards(): pl.pallas_call(functools.partial(scale, rows), out_shape=jax.ShapeDtypeSt...]
where the time goes in v2:
time: 191 us; the launch traced here: 190 us
  Pallas kernels  186 us (97%)
  local copies, waits for them, and re-layouts  1.93 us (1%)
    pallas_call x1, Pallas kernels, shards(): pl.pallas_call(functools.partial(kernel, n_dp, n_t, chunks, float(d_all),...  179 us
    pallas_call x1, Pallas kernels, shards(): pl.pallas_call(functools.partial(scale, rows), out_shape=jax.ShapeDtypeSt...  6.38 us

profile of v2, /device:TPU:0, one launch (start us, length us, event | category | flops | bytes accessed | tf_op | source)
XLA Modules:
  0.0 190.3 jit_solution(2627414549987784342)
XLA Ops:
  0.6 1.3 reshape.21.column_state
  2.0 179.5 %shard_map.84 = (f32[1024,3584]{1,0:T(8,128)S(1)}, f32[1,1024]{1,0:T(1,128)}, f32[1,3584]{1,0:T(1,128)}, f32[1024,128]{1,0:T(8,128)S(1)}, f32[1,3584]{1,0:T(1,128)S(1)}, /*index=5*/f32[1,128]{1,0:T(1,128)}) custom-call(bf16[64,8192]{1,0:T(8,128)(2,1)} %cot.1, bf16[256,3584]{1,0:T(8,128)(2,1)} %gate_in.1, bf16[256,3584]{1,0:T(8,128)(2,1)} %up_in.1, ...), custom_call_target="tpu_custom_call" | custom-call | tf_op jit(solution)/shard_map/pallas_call | solution.py:387
  181.5 0.0 copy-start
  181.5 0.0 copy-start.1
  181.5 0.0 copy-start.2
  181.5 6.4 %shard_map.85 = f32[1024,3584]{1,0:T(8,128)} custom-call(f32[1024,3584]{1,0:T(8,128)S(1)} %get-tuple-element.10.grad, f32[1024,128]{1,0:T(8,128)S(1)} %get-tuple-element.11.rfac, f32[1,3584]{1,0:T(1,128)S(1)} %get-tuple-element.12.cfac), custom_call_target="tpu_custom_call" | custom-call | tf_op jit(solution)/shard_map/pallas_call | solution.py:421
  187.9 0.0 copy-done
  187.9 0.6 reduce
  188.5 0.0 copy-done.1
  188.5 0.6 copy.11
  189.1 0.0 copy-done.2
Async XLA Ops:
  181.5 6.4 %copy-start = (f32[1,3584]{1,0:T(1,128)S(1)}, f32[1,3584]{1,0:T(1,128)}, u32[]{:S(2)}) copy-start(f32[1,3584]{1,0:T(1,128)} %get-tuple-element.14) | copy-start | bytes 43012
  181.5 7.0 %copy-start.1 = (f32[1,1024]{1,0:T(1,128)S(1)}, f32[1,1024]{1,0:T(1,128)}, u32[]{:S(2)}) copy-start(f32[1,1024]{1,0:T(1,128)} %get-tuple-element.13) | copy-start | bytes 12292
  181.5 7.6 %copy-start.2 = (f32[1,128]{1,0:T(1,128)S(1)}, f32[1,128]{1,0:T(1,128)}, u32[]{:S(2)}) copy-start(f32[1,128]{1,0:T(1,128)} %get-tuple-element.15) | copy-start | bytes 1540
